TPU v7x, 32 devices: a whole 2x2x4 slice. The times are simulated.
32 devices in a mesh: seq: 16 (over z, y, x), head: 2 (over core).
Axes of the slice: x: 2, y: 2, z: 4, core: 2. Of those that a mesh axis runs over, the one named last changes fastest.
Arguments:
- queries: bfloat16 [4096, 32, 128], P('seq', 'head'), may hold values from -8 to 8
- keys: bfloat16 [4096, 8, 128], P('seq', 'head'), may hold values from -8 to 8
- values: bfloat16 [4096, 8, 128], P('seq', 'head'), may hold values from -6 to 6
- out_weight: bfloat16 [4096, 4096], P('head', 'seq'), may hold values from -0.125 to 0.125
- doc_lengths: int32 [16], replicated, may hold values from 1 to 2304, 4096 in all
Outputs:
- projected: bfloat16 [4096, 4096], P('seq', 'head')
Inputs may be any that keep to these rules, and one draw needn't show every extreme that they name: `doc_lengths`: every document is at most 2304 tokens long and the longest is exactly that; the lengths sum to 4096.
All inputs are finite; a program needn't handle non-finite values.
Results may differ from a plain program's by a relative error of at most 0.014.
Values may be sent and summed in bfloat16 or wider, within the bound.
A program may use at most 64 MiB of HBM per device.

v0:
```python
import functools
import math

import jax
import jax.numpy as jnp
from jax import lax
from jax.experimental import pallas as pl
from jax.experimental.pallas import tpu as pltpu
from jax.sharding import PartitionSpec as P

MESH = pl.DeviceIdType.MESH


def kernel(
    shape,
    q_in, k_in, v_in, w_ref, lo_ref, out_ref,
    q_ref, k_ref, v_ref,
    q_all, k_all, v_all, w_all, a_all, acc, row_max, row_total, partial, peer, summed, result,
    q_send, q_recv, k_send, k_recv, v_send, v_recv, kz_send, kz_recv, vz_send, vz_recv,
    up_send, up_recv, down_send, down_recv, a_send, a_recv, p_send, p_recv, c_send, c_recv, local_sem,
):
    inner, outer, heads, group, back, span, last = shape
    tok, width = k_in.shape[0], k_in.shape[2]
    part_rows = group * width
    share = outer // heads
    seq, head = lax.axis_index("seq"), lax.axis_index("head")
    o, i = seq // inner, seq % inner

    def remote(src, dst, send, recv, device):
        return pltpu.make_async_remote_copy(
            src_ref=src, dst_ref=dst, send_sem=send, recv_sem=recv, device_id=device, device_id_type=MESH
        )

    def mate(d):
        return (i + d) % inner

    def plane(d):
        return {"seq": o * inner + mate(d)}

    above, below = {"seq": jnp.minimum(seq + inner, outer * inner - 1)}, {"seq": jnp.maximum(seq - inner, 0)}
    has_above, has_below = o + 1 < outer, o >= 1

    barrier = pltpu.get_barrier_semaphore()
    for d in range(1, inner):
        pl.semaphore_signal(barrier, inc=1, device_id=plane(d), device_id_type=MESH)
    for d in range(1, heads):
        pl.semaphore_signal(barrier, inc=1, device_id={"head": (head + d) % heads}, device_id_type=MESH)

    @pl.when(has_above)
    def _():
        pl.semaphore_signal(barrier, inc=1, device_id=above, device_id_type=MESH)

    @pl.when(has_below)
    def _():
        pl.semaphore_signal(barrier, inc=1, device_id=below, device_id_type=MESH)

    pl.semaphore_wait(
        barrier, inner - 1 + heads - 1 + has_above.astype(jnp.int32) + has_below.astype(jnp.int32)
    )

    def kv_copies(d):
        return (
            remote(k_ref.at[mate(d)], k_all.at[0, i], k_send.at[d], k_recv.at[d], plane(d)),
            remote(v_ref.at[mate(d)], v_all.at[0, i], v_send.at[d], v_recv.at[d], plane(d)),
        )

    def q_copy(d):
        return remote(q_ref.at[mate(d)], q_all.at[i], q_send.at[d], q_recv.at[d], plane(d))

    def up_copy(t, first):
        return remote(
            w_ref if first else w_all.at[jnp.maximum(o - t + 1, 0)],
            w_all.at[jnp.maximum(o - t + 1, 0)], up_send.at[t], up_recv.at[t], above,
        )

    def down_copy(t, first):
        return remote(
            w_ref if first else w_all.at[jnp.minimum(o + t - 1, outer - 1)],
            w_all.at[jnp.minimum(o + t - 1, outer - 1)], down_send.at[t], down_recv.at[t], below,
        )

    def got_up(t):
        @pl.when(o >= t)
        def _():
            slot = w_all.at[jnp.maximum(o - t, 0)]
            remote(slot, slot, up_send.at[t], up_recv.at[t], below).wait_recv()

    def got_down(t):
        @pl.when(o + t < outer)
        def _():
            slot = w_all.at[jnp.minimum(o + t, outer - 1)]
            remote(slot, slot, down_send.at[t], down_recv.at[t], above).wait_recv()

    def go_up(t, first=False):
        @pl.when(has_above & (o >= t - 1))
        def _():
            up_copy(t, first).start()

    def go_down(t, first=False):
        @pl.when(has_below & (o + t - 1 < outer))
        def _():
            down_copy(t, first).start()

    if outer > 1:
        go_up(1, True)
        go_down(1, True)
    k_ref[...] = jnp.swapaxes(k_in[...], 0, 1)
    by_head = jnp.swapaxes(v_in[...], 0, 1)
    for j in range(inner):
        v_ref[j] = by_head[j].T
    by_head = jnp.swapaxes(q_in[...], 0, 1)
    for j in range(inner * group):
        q_ref[j // group, :, (j % group) * tok : (j % group + 1) * tok] = by_head[j].T
    for d in range(1, inner):
        for copy in kv_copies(d):
            copy.start()
    for d in range(1, inner):
        q_copy(d).start()

    locals_ = [
        pltpu.make_async_copy(q_ref.at[i], q_all.at[i], local_sem.at[0]),
        pltpu.make_async_copy(k_ref.at[i], k_all.at[0, i], local_sem.at[1]),
        pltpu.make_async_copy(v_ref.at[i], v_all.at[0, i], local_sem.at[2]),
        pltpu.make_async_copy(w_ref, w_all.at[o], local_sem.at[3]),
    ]
    for copy in locals_:
        copy.start()
    for copy in locals_:
        copy.wait()

    def from_mate(d):
        return (i + inner - d) % inner

    for d in range(1, inner):
        k_slot, v_slot = k_all.at[0, from_mate(d)], v_all.at[0, from_mate(d)]
        remote(k_slot, k_slot, k_send.at[d], k_recv.at[d], plane(d)).wait_recv()
        remote(v_slot, v_slot, v_send.at[d], v_recv.at[d], plane(d)).wait_recv()

    def slot_of(ref, b, only_last):
        return ref.at[b, pl.ds(inner - last, last)] if only_last else ref.at[b]

    def lift(b, only_last):
        return (
            remote(slot_of(k_all, b, only_last), slot_of(k_all, b + 1, only_last), kz_send.at[b], kz_recv.at[b + 1], above),
            remote(slot_of(v_all, b, only_last), slot_of(v_all, b + 1, only_last), vz_send.at[b], vz_recv.at[b + 1], above),
        )

    def start_lift(b, only_last):
        @pl.when(has_above & (o >= b))
        def _():
            for copy in lift(b, only_last):
                copy.start()

    def got_lift(b, only_last):
        k_slot, v_slot = slot_of(k_all, b, only_last), slot_of(v_all, b, only_last)
        remote(k_slot, k_slot, kz_send.at[b], kz_recv.at[b], below).wait_recv()
        remote(v_slot, v_slot, vz_send.at[b], vz_recv.at[b], below).wait_recv()

    if back >= 1:
        start_lift(0, back == 1)
    row_max[...] = jnp.full(row_max.shape, -1e30, jnp.float32)
    row_total[...] = jnp.zeros(row_total.shape, jnp.float32)
    acc[...] = jnp.zeros(acc.shape, jnp.float32)
    factor = math.log2(math.e) / math.sqrt(width)

    def tile(b, qb, kb, diagonal):
        key_pos = ((o - b) * inner + kb) * tok + lax.broadcasted_iota(jnp.int32, (tok, tok), 0)
        allowed = key_pos >= lo_ref[qb]
        if diagonal:
            allowed &= lax.broadcasted_iota(jnp.int32, (tok, tok), 0) <= lax.broadcasted_iota(
                jnp.int32, (tok, tok), 1
            )
        keys_here, values_here = k_all[b, kb], v_all[b, kb]
        for r in range(group):
            cols = pl.ds(r * tok, tok)
            scores = jnp.dot(keys_here, q_all[qb, :, cols], preferred_element_type=jnp.float32)
            scores = jnp.where(allowed, scores * factor, -1e30)
            old_max = row_max[qb, :, cols]
            new_max = jnp.maximum(old_max, jnp.max(scores, axis=0, keepdims=True))
            weights = jnp.exp2(scores - new_max)
            rescale = jnp.exp2(old_max - new_max)
            row_max[qb, :, cols] = new_max
            row_total[qb, :, cols] = row_total[qb, :, cols] * rescale + jnp.sum(weights, axis=0, keepdims=True)
            acc[qb, :, cols] = acc[qb, :, cols] * rescale + jnp.dot(
                values_here, weights.astype(jnp.bfloat16), preferred_element_type=jnp.float32
            )

    def own_rows(qb, carry):
        tile(0, qb, qb, True)

        def own_keys(kb, inside):
            tile(0, qb, kb, False)
            return inside

        return lax.fori_loop(0, qb, own_keys, carry)

    own_rows(i, 0)
    for d in range(1, inner):
        q_slot = q_all.at[from_mate(d)]
        remote(q_slot, q_slot, q_send.at[d], q_recv.at[d], plane(d)).wait_recv()
        own_rows(from_mate(d), 0)

    def attend(b, qb):
        def cols(kb, inside):
            tile(b, qb, kb, False)
            return inside

        lax.fori_loop(jnp.maximum(b * inner + qb - span, 0), inner, cols, 0)

    def middle(b):
        @pl.when(o >= b)
        def _():
            got_lift(b, False)

        @pl.when(has_above & (o >= b))
        def _():
            for copy in lift(b, False):
                copy.start()

    if outer > 1:
        got_down(1)
    if outer > 2:
        go_down(2)
    def whole_slot(b, carry):
        middle(b)
        return carry

    if back > 2:
        middle(1)
    elif back == 2:
        @pl.when(o >= 1)
        def _():
            got_lift(1, False)

        start_lift(1, True)
    elif back == 1:
        @pl.when(o >= 1)
        def _():
            got_lift(1, True)
    early = inner // 2 if back > 1 else 0

    def early_rows(qb, carry):
        attend(1, qb)
        return carry

    if early:
        @pl.when(o >= 1)
        def _():
            lax.fori_loop(inner - early, inner, early_rows, 0)

    if back > 2:
        lax.fori_loop(2, back - 1, whole_slot, 0)

        @pl.when(o >= back - 1)
        def _():
            got_lift(back - 1, False)

        start_lift(back - 1, True)
    if outer > 1:
        got_up(1)
    if outer > 2:
        go_up(2)

    def a_copy(qb, d):
        slot = a_all.at[qb, i]
        return remote(slot, slot, a_send.at[qb, d], a_recv.at[qb, d], plane(d))

    def send_rows(qb):
        for d in range(1, inner):
            a_copy(qb, d).start()

    def finish(qb):
        for r in range(group):
            cols = pl.ds(r * tok, tok)
            normal = acc[qb, :, cols] / row_total[qb, :, cols]
            a_all[qb, i, :, r * width : (r + 1) * width] = normal.T.astype(jnp.bfloat16)

    deepest = min(inner, span + inner - back * inner)

    def finish_rows(k, carry):
        qb = inner - 1 - k

        def slots(b, inside):
            attend(b, qb)
            return inside

        lax.fori_loop(jnp.where(k < early, 2, 1), jnp.minimum(o, back - 1) + 1, slots, 0)
        if back > 1:
            @pl.when((o >= back) & (qb == deepest - 1))
            def _():
                got_lift(back, True)

        if back >= 1:
            @pl.when((o >= back) & (qb < deepest))
            def _():
                attend(back, qb)

        finish(qb)
        send_rows(qb)
        return carry

    lax.fori_loop(0, inner, finish_rows, 0)

    def hop(t, carry):
        got_down(t - 1)
        go_down(t)
        got_up(t - 1)
        go_up(t)
        return carry

    if outer > 3:
        got_down(2)
        go_down(3)
        got_up(2)
        go_up(3)
        lax.fori_loop(4, outer, hop, 0)
    def multiply(qb, s):
        value = jnp.dot(a_all[qb, 0], w_all[s, 0:part_rows, :], preferred_element_type=jnp.float32)
        for j in range(1, inner):
            value += jnp.dot(
                a_all[qb, j], w_all[s, j * part_rows : (j + 1) * part_rows, :], preferred_element_type=jnp.float32
            )
        partial[s, qb] = value.astype(jnp.bfloat16)

    def p_copy(s):
        to = s // share
        d = (to + heads - head) % heads
        return remote(
            partial.at[s], peer.at[d, s % share], p_send.at[s], p_recv.at[d, s % share], {"head": to}
        )

    def give(s):
        @pl.when(s // share != head)
        def _():
            p_copy(s).start()

    def c_copy(sl, d):
        return remote(summed.at[sl, mate(d)], result.at[sl, i], c_send.at[sl, d], c_recv.at[sl, d], plane(d))

    def absorb(s):
        @pl.when(s // share == head)
        def _():
            sl = s % share
            for d in range(1, heads):
                slot = peer.at[d, sl]
                remote(slot, slot, p_send.at[s], p_recv.at[d, sl], {"head": (head + d) % heads}).wait_recv()

            def rows(j, carry):
                total = partial[s, j].astype(jnp.float32)
                for d in range(1, heads):
                    total = total + peer[d, sl, j].astype(jnp.float32)
                summed[sl, j] = total.astype(jnp.bfloat16)
                return carry

            lax.fori_loop(0, inner, rows, 0)
            for d in range(1, inner):
                c_copy(sl, d).start()
            result[sl, i] = summed[sl, i]

    def near(t, act):
        @pl.when(o - t >= 0)
        def _():
            act(jnp.maximum(o - t, 0))

        @pl.when((o + t < outer) & (t > 0))
        def _():
            act(jnp.minimum(o + t, outer - 1))

    near_count = max(outer - 1, 1)

    def got_rows(qb):
        for d in range(1, inner):
            slot = a_all.at[qb, from_mate(d)]
            remote(slot, slot, a_send.at[qb, d], a_recv.at[qb, d], plane(d)).wait_recv()

    def early_blocks(k, carry):
        qb = inner - 1 - k
        got_rows(qb)

        def shards(t, inside):
            near(t, lambda s: multiply(qb, s))
            return inside

        lax.fori_loop(0, near_count, shards, 0)
        return carry

    lax.fori_loop(0, inner - 1, early_blocks, 0)
    got_rows(0)

    def final_block(t, carry):
        def act(s):
            multiply(0, s)
            give(s)

        near(t, act)

        @pl.when(t >= 1)
        def _():
            near(t - 1, absorb)

        return carry

    lax.fori_loop(0, near_count, final_block, 0)
    near(near_count - 1, absorb)
    if outer > 1:
        if outer > 2:
            got_down(outer - 1)
            got_up(outer - 1)

        def far(s):
            def rows(qb, carry):
                multiply(qb, s)
                return carry

            lax.fori_loop(0, inner, rows, 0)
            give(s)

        near(outer - 1, far)
        near(outer - 1, absorb)
    for sl in range(share):
        for d in range(1, inner):
            slot = result.at[sl, from_mate(d)]
            remote(slot, slot, c_send.at[sl, d], c_recv.at[sl, d], plane(d)).wait_recv()
    wide = out_ref.shape[1] // (share * inner)
    for s in range(share):
        for j in range(inner):
            out_ref[:, (s * inner + j) * wide : (s * inner + j + 1) * wide] = result[s, j]

    for d in range(1, inner):
        for copy in kv_copies(d):
            copy.wait_send()
        q_copy(d).wait_send()
        for qb in range(inner):
            a_copy(qb, d).wait_send()
        for sl in range(share):
            c_copy(sl, d).wait_send()

    def given(s, carry):
        @pl.when(s // share != head)
        def _():
            p_copy(s).wait_send()

        return carry

    lax.fori_loop(0, outer, given, 0)

    def lift_done(b, only_last):
        @pl.when(has_above & (o >= b))
        def _():
            for copy in lift(b, only_last):
                copy.wait_send()

    if back > 1:
        def lift_sent(b, carry):
            lift_done(b, False)
            return carry

        lax.fori_loop(0, back - 1, lift_sent, 0)
    if back >= 1:
        lift_done(back - 1, True)

    def hop_sent(t, first):
        @pl.when(has_above & (o >= t - 1))
        def _():
            up_copy(t, first).wait_send()

        @pl.when(has_below & (o + t - 1 < outer))
        def _():
            down_copy(t, first).wait_send()

    def later_sent(t, carry):
        hop_sent(t, False)
        return carry

    if outer > 1:
        hop_sent(1, True)
        lax.fori_loop(2, outer, later_sent, 0)


def body(queries, keys, values, out_weight, doc_lengths):
    tok, heads_here, width = queries.shape
    inner = keys.shape[1]
    group = heads_here // inner
    count = lax.axis_size("seq")
    heads = lax.axis_size("head")
    outer = count // inner
    span = count // 2 + 1
    plane_rows = inner * tok
    reach = span * tok - 1
    back = min(outer - 1, -(-reach // plane_rows))
    last = min(inner, -(-(reach - (back - 1) * plane_rows) // tok))
    share = outer // heads
    depth, wide = out_weight.shape

    positions = (lax.axis_index("seq") // inner) * plane_rows + jnp.arange(plane_rows, dtype=jnp.int32)
    ends = jnp.cumsum(doc_lengths)
    starts = jnp.max(jnp.where(ends[None, :] <= positions[:, None], ends[None, :], 0), axis=1)
    starts = starts.reshape(inner, 1, tok)

    bf16, f32 = jnp.bfloat16, jnp.float32
    dma = pltpu.SemaphoreType.DMA
    scratch = [
        pltpu.VMEM((inner, width, group * tok), bf16),
        pltpu.VMEM((inner, tok, width), bf16),
        pltpu.VMEM((inner, width, tok), bf16),
        pltpu.VMEM((inner, width, group * tok), bf16),
        pltpu.VMEM((back + 1, inner, tok, width), bf16),
        pltpu.VMEM((back + 1, inner, width, tok), bf16),
        pltpu.VMEM((outer, depth, wide), bf16),
        pltpu.VMEM((inner, inner, tok, group * width), bf16),
        pltpu.VMEM((inner, width, group * tok), f32),
        pltpu.VMEM((inner, 1, group * tok), f32),
        pltpu.VMEM((inner, 1, group * tok), f32),
        pltpu.VMEM((outer, inner, tok, wide), bf16),
        pltpu.VMEM((heads, share, inner, tok, wide), bf16),
        pltpu.VMEM((share, inner, tok, wide), bf16),
        pltpu.VMEM((share, inner, tok, wide), bf16),
    ]
    scratch += [dma((inner,))] * 6 + [dma((back + 1,))] * 4 + [dma((outer,))] * 4
    scratch += [dma((inner, inner))] * 2 + [dma((outer,)), dma((heads, share))] + [dma((share, inner))] * 2 + [dma((4,))]
    shape = (inner, outer, heads, group, back, span, last)
    return pl.pallas_call(
        functools.partial(kernel, shape),
        out_shape=jax.ShapeDtypeStruct((tok, share * inner * wide), bf16),
        in_specs=[pl.BlockSpec(memory_space=pltpu.VMEM)] * 5,
        out_specs=pl.BlockSpec(memory_space=pltpu.VMEM),
        scratch_shapes=scratch,
        compiler_params=pltpu.CompilerParams(
            collective_id=0, has_side_effects=True, vmem_limit_bytes=60 * 1024 * 1024
        ),
    )(queries, keys, values, out_weight, starts)


def solution(mesh):
    placed = (
        P("seq", "head", None),
        P("seq", "head", None),
        P("seq", "head", None),
        P("head", "seq"),
        P(),
    )
    return jax.shard_map(
        body, mesh=mesh, in_specs=placed, out_specs=P("seq", "head"), check_vma=False
    )
```

profile of v0, /device:TPU:24, one launch (start us, length us, event | category | flops | bytes accessed | tf_op | source)
XLA Modules:
  0.0 120.0 jit_solution(13372499873713555263)
XLA Ops:
  0.0 0.0 copy-start
  0.0 0.6 copy-done
  0.7 0.1 copy.8
  0.8 0.1 reduce
  0.9 0.7 select_reduce_fusion
  1.6 116.1 %shard_map.55 = bf16[256,2048]{1,0:T(8,128)(2,1)} custom-call(bf16[256,16,128]{2,1,0:T(8,128)(2,1)} %q_in.1, bf16[256,4,128]{2,1,0:T(4,128)(2,1)} %k_in.1, bf16[256,4,128]{2,1,0:T(4,128)(2,1)} %v_in.1, bf16[2048,256]{1,0:T(8,128)(2,1)} %w_ref.1, s32[4,1,256]{2,1,0:T(1,128)} %bitcast.2), custom_call_target="tpu_custom_call" | custom-call | tf_op jit(solution)/shard_map/pallas_call | solution.py:522
  117.7 2.3 %copy.10 = bf16[256,2048]{1,0:T(8,128)(2,1)} copy(bf16[256,2048]{1,0:T(8,128)(2,1)} %shard_map.55) | data formatting | bytes 2097152
  (2 shorter events, 0.0 us)
Async XLA Ops:
  0.0 0.7 copy-start
where the time goes:
time: 120 us
  Pallas kernels  116 us (97%)
  local copies, waits for them, and re-layouts  3.04 us (3%)
    pallas_call x1, Pallas kernels, body(): pl.pallas_call(functools.partial(kernel, shape), out_shape=jax.ShapeDtype...  116 us
    unnamed x3, local copies, waits for them, and re-layouts  2.96 us

commit v1 on v0

--- a/solution.py
+++ b/solution.py
@@ -475,6 +475,424 @@
     if outer > 1:
         hop_sent(1, True)
         lax.fori_loop(2, outer, later_sent, 0)
+
+
+def paired_kernel(
+    shape,
+    q_in, k_in, v_in, w_ref, lo_ref, out_ref,
+    q_ref, k_ref, v_ref,
+    q_all, k_all, v_all, w_all, a_all, acc, row_max, row_total, part, peer, first_in, second_in, final, final_in,
+    q_send, q_recv, k_send, k_recv, v_send, v_recv, kz_send, kz_recv, vz_send, vz_recv,
+    w_send, w_recv, f_send, f_recv, a_send, a_recv, d_send, d_recv,
+    r_send, r_recv, s_send, s_recv, o_send, o_recv, local_sem,
+):
+    inner, outer, heads, group, back, span, last = shape
+    tok, width = k_in.shape[0], k_in.shape[2]
+    rows = group * width
+    wide = w_ref.shape[1]
+    half = (inner // 2) * wide
+    seq, head = lax.axis_index("seq"), lax.axis_index("head")
+    o, i = seq // inner, seq % inner
+    ix, iy = i % 2, i // 2
+    low, high = o % 2, o // 2
+    kept = (head + high) % 2
+
+    def remote(src, dst, send, recv, device):
+        return pltpu.make_async_remote_copy(
+            src_ref=src, dst_ref=dst, send_sem=send, recv_sem=recv, device_id=device, device_id_type=MESH
+        )
+
+    def mate(d):
+        return (i + d) % inner
+
+    def from_mate(d):
+        return (i + inner - d) % inner
+
+    def plane(d):
+        return {"seq": o * inner + mate(d)}
+
+    across = ({"seq": o * inner + iy * 2 + 1 - ix}, {"seq": o * inner + (1 - iy) * 2 + ix})
+    pair = {"seq": (o + 1 - 2 * low) * inner + i}
+    far = {"seq": ((o + 2) % outer) * inner + i}
+    other = {"head": (head + 1) % heads}
+    above, below = {"seq": jnp.minimum(seq + inner, outer * inner - 1)}, {"seq": jnp.maximum(seq - inner, 0)}
+    has_above, has_below = o + 1 < outer, o >= 1
+
+    barrier = pltpu.get_barrier_semaphore()
+    for d in range(1, inner):
+        pl.semaphore_signal(barrier, inc=1, device_id=plane(d), device_id_type=MESH)
+    pl.semaphore_signal(barrier, inc=1, device_id=other, device_id_type=MESH)
+    pl.semaphore_signal(barrier, inc=1, device_id=far, device_id_type=MESH)
+
+    @pl.when(has_above)
+    def _():
+        pl.semaphore_signal(barrier, inc=1, device_id=above, device_id_type=MESH)
+
+    @pl.when(has_below)
+    def _():
+        pl.semaphore_signal(barrier, inc=1, device_id=below, device_id_type=MESH)
+
+    pl.semaphore_wait(barrier, inner + 1 + has_above.astype(jnp.int32) + has_below.astype(jnp.int32))
+
+    def kv_copies(d):
+        return (
+            remote(k_ref.at[mate(d)], k_all.at[0, i], k_send.at[d], k_recv.at[d], plane(d)),
+            remote(v_ref.at[mate(d)], v_all.at[0, i], v_send.at[d], v_recv.at[d], plane(d)),
+        )
+
+    def q_copy(d):
+        return remote(q_ref.at[mate(d)], q_all.at[i], q_send.at[d], q_recv.at[d], plane(d))
+
+    def w_rows(j):
+        return w_ref.at[pl.ds(pl.multiple_of(j * rows, rows), rows)]
+
+    def w_copy(d):
+        return remote(w_rows(mate(d)), w_all.at[0, i], w_send.at[d], w_recv.at[d], plane(d))
+
+    def far_copy(d):
+        src = w_rows(i) if d == 0 else w_all.at[0, from_mate(d)]
+        return remote(src, w_all.at[1, from_mate(d)], f_send.at[d], f_recv.at[d], far)
+
+    far_copy(0).start()
+    k_ref[...] = jnp.swapaxes(k_in[...], 0, 1)
+    for d in range(1, inner):
+        kv_copies(d)[0].start()
+    by_head = jnp.swapaxes(v_in[...], 0, 1)
+    for j in range(inner):
+        v_ref[j] = by_head[j].T
+    for d in range(1, inner):
+        kv_copies(d)[1].start()
+    by_head = jnp.swapaxes(q_in[...], 0, 1)
+    for j in range(inner * group):
+        q_ref[j // group, :, (j % group) * tok : (j % group + 1) * tok] = by_head[j].T
+    for d in range(1, inner):
+        q_copy(d).start()
+    for d in range(1, inner):
+        w_copy(d).start()
+
+    locals_ = [
+        pltpu.make_async_copy(q_ref.at[i], q_all.at[i], local_sem.at[0]),
+        pltpu.make_async_copy(k_ref.at[i], k_all.at[0, i], local_sem.at[1]),
+        pltpu.make_async_copy(v_ref.at[i], v_all.at[0, i], local_sem.at[2]),
+        pltpu.make_async_copy(w_rows(i), w_all.at[0, i], local_sem.at[3]),
+    ]
+    for copy in locals_:
+        copy.start()
+    row_max[...] = jnp.full(row_max.shape, -1e30, jnp.float32)
+    row_total[...] = jnp.zeros(row_total.shape, jnp.float32)
+    acc[...] = jnp.zeros(acc.shape, jnp.float32)
+    for copy in locals_:
+        copy.wait()
+
+    for d in range(1, inner):
+        k_slot, v_slot = k_all.at[0, from_mate(d)], v_all.at[0, from_mate(d)]
+        remote(k_slot, k_slot, k_send.at[d], k_recv.at[d], plane(d)).wait_recv()
+        remote(v_slot, v_slot, v_send.at[d], v_recv.at[d], plane(d)).wait_recv()
+
+    def slot_of(ref, b, only_last):
+        return ref.at[b, pl.ds(inner - last, last)] if only_last else ref.at[b]
+
+    def lift(b):
+        only_last = b == back - 1
+        return (
+            remote(slot_of(k_all, b, only_last), slot_of(k_all, b + 1, only_last), kz_send.at[b], kz_recv.at[b + 1], above),
+            remote(slot_of(v_all, b, only_last), slot_of(v_all, b + 1, only_last), vz_send.at[b], vz_recv.at[b + 1], above),
+        )
+
+    def start_lift(b):
+        @pl.when(has_above & (o >= b))
+        def _():
+            for copy in lift(b):
+                copy.start()
+
+    def got_lift(b):
+        @pl.when(o >= b)
+        def _():
+            k_slot, v_slot = slot_of(k_all, b, b == back), slot_of(v_all, b, b == back)
+            remote(k_slot, k_slot, kz_send.at[b], kz_recv.at[b], below).wait_recv()
+            remote(v_slot, v_slot, vz_send.at[b], vz_recv.at[b], below).wait_recv()
+
+    if back >= 1:
+        start_lift(0)
+    factor = math.log2(math.e) / math.sqrt(width)
+
+    def tile(b, qb, kb, diagonal):
+        key_pos = ((o - b) * inner + kb) * tok + lax.broadcasted_iota(jnp.int32, (tok, tok), 0)
+        allowed = key_pos >= lo_ref[qb]
+        if diagonal:
+            allowed &= lax.broadcasted_iota(jnp.int32, (tok, tok), 0) <= lax.broadcasted_iota(
+                jnp.int32, (tok, tok), 1
+            )
+        keys_here, values_here = k_all[b, kb], v_all[b, kb]
+        raw = [
+            jnp.dot(keys_here, q_all[qb, :, r * tok : (r + 1) * tok], preferred_element_type=jnp.float32)
+            for r in range(group)
+        ]
+        for r in range(group):
+            cols = pl.ds(r * tok, tok)
+            scores = jnp.where(allowed, raw[r] * factor, -1e30)
+            old_max = row_max[qb, :, cols]
+            new_max = jnp.maximum(old_max, jnp.max(scores, axis=0, keepdims=True))
+            weights = jnp.exp2(scores - new_max)
+            rescale = jnp.exp2(old_max - new_max)
+            row_max[qb, :, cols] = new_max
+            row_total[qb, :, cols] = row_total[qb, :, cols] * rescale + jnp.sum(weights, axis=0, keepdims=True)
+            acc[qb, :, cols] = acc[qb, :, cols] * rescale + jnp.dot(
+                values_here, weights.astype(jnp.bfloat16), preferred_element_type=jnp.float32
+            )
+
+    def own_rows(qb):
+        tile(0, qb, qb, True)
+
+        def own_keys(kb, inside):
+            tile(0, qb, kb, False)
+            return inside
+
+        lax.fori_loop(0, qb, own_keys, 0)
+
+    def attend(b, qb):
+        def cols(kb, inside):
+            tile(b, qb, kb, False)
+            return inside
+
+        lax.fori_loop(jnp.maximum(b * inner + qb - span, 0), inner, cols, 0)
+
+    def own_from(d, carry):
+        @pl.when(d >= 1)
+        def _():
+            q_slot = q_all.at[from_mate(d)]
+            remote(q_slot, q_slot, q_send.at[d], q_recv.at[d], plane(d)).wait_recv()
+
+        own_rows(from_mate(d))
+        return carry
+
+    lax.fori_loop(0, inner, own_from, 0)
+
+    def rows_of(b, begin, end):
+        def one(k, carry):
+            attend(b, inner - 1 - k)
+            return carry
+
+        @pl.when(o >= b)
+        def _():
+            lax.fori_loop(begin, end, one, 0)
+
+    if back > 1:
+        got_lift(1)
+        start_lift(1)
+        rows_of(1, 0, inner // 2)
+    for d in range(1, inner):
+        slot = w_all.at[0, from_mate(d)]
+        remote(slot, slot, w_send.at[d], w_recv.at[d], plane(d)).wait_recv()
+        far_copy(d).start()
+    if back > 1:
+        rows_of(1, inner // 2, inner)
+    for b in range(2, back):
+        got_lift(b)
+        start_lift(b)
+        if b < back - 1:
+            rows_of(b, 0, inner)
+
+    def a_copy(qb):
+        return remote(a_all.at[0, qb], a_all.at[1, qb], a_send.at[qb], a_recv.at[qb], pair)
+
+    def finish(qb):
+        for r in range(group):
+            cols = pl.ds(r * tok, tok)
+            normal = acc[qb, :, cols] / row_total[qb, :, cols]
+            a_all[0, qb, :, r * width : (r + 1) * width] = normal.T.astype(jnp.bfloat16)
+
+    def give(qb, side):
+        return remote(part.at[side, qb], peer.at[qb], d_send.at[qb], d_recv.at[qb], other)
+
+    def multiply(side, qb):
+        if side == 0:
+            slot = a_all.at[1, qb]
+            remote(slot, slot, a_send.at[qb], a_recv.at[qb], pair).wait_recv()
+        for p in range(2):
+            for m in range(inner):
+                value = jnp.dot(a_all[p, qb], w_all[side, m], preferred_element_type=jnp.float32)
+                c, mm = m // 2, m % 2
+                part[side, qb, c, p, :, mm * wide : (mm + 1) * wide] = value.astype(jnp.bfloat16)
+
+        @pl.when(kept != side)
+        def _():
+            give(qb, side).start()
+
+    def first_copy(qb, c):
+        t = (qb // 2) if c == 0 else (qb % 2)
+        return remote(part.at[kept, qb, c], first_in.at[c, t], r_send.at[c, t], r_recv.at[c, t], across[c])
+
+    def is_sent(qb, c):
+        return (qb % 2 != ix) if c == 0 else (qb // 2 != iy)
+
+    def combine(qb):
+        slot = peer.at[qb]
+        remote(slot, slot, d_send.at[qb], d_recv.at[qb], other).wait_recv()
+        for c in range(2):
+            total = part[kept, qb, c].astype(jnp.float32) + peer[qb, c].astype(jnp.float32)
+            part[kept, qb, c] = total.astype(jnp.bfloat16)
+
+            @pl.when(is_sent(qb, c))
+            def _():
+                first_copy(qb, c).start()
+
+    def kept_block(c, t):
+        return 2 * t + ix if c == 0 else 2 * iy + t
+
+    def second_copy(c, t):
+        return remote(part.at[kept, kept_block(c, t), c], second_in.at[c], s_send.at[c], s_recv.at[c], across[1 - c])
+
+    def first_sum(c, t):
+        slot = first_in.at[c, t]
+        remote(slot, slot, r_send.at[c, t], r_recv.at[c, t], across[c]).wait_recv()
+        qb = kept_block(c, t)
+        total = part[kept, qb, c].astype(jnp.float32) + first_in[c, t].astype(jnp.float32)
+        part[kept, qb, c] = total.astype(jnp.bfloat16)
+
+        @pl.when(t != (iy if c == 0 else ix))
+        def _():
+            second_copy(c, t).start()
+
+    def first_sums():
+        for t in (1, 0):
+            for c in range(2):
+                first_sum(c, t)
+
+    def out_copy(c):
+        return remote(final.at[c], final_in.at[c], o_send.at[c], o_recv.at[c], pair)
+
+    def columns(parity, c):
+        return pl.ds(pl.multiple_of(parity * (2 * half) + c * half, half), half)
+
+    def second_sum(c):
+        slot = second_in.at[c]
+        remote(slot, slot, s_send.at[c], s_recv.at[c], across[1 - c]).wait_recv()
+        total = part[kept, i, c].astype(jnp.float32) + second_in[c].astype(jnp.float32)
+        total = total.astype(jnp.bfloat16)
+        final[c] = total[1]
+        out_copy(c).start()
+        out_ref[:, columns(low, c)] = total[0]
+
+    deepest = min(inner, span + inner - back * inner)
+
+    def finish_rows(k, carry):
+        qb = inner - 1 - k
+
+        @pl.when(o >= back - 1)
+        def _():
+            if back > 2:
+                attend(back - 1, qb)
+
+        @pl.when((o >= back) & (qb == deepest - 1))
+        def _():
+            got_lift(back)
+
+        @pl.when((o >= back) & (qb < deepest))
+        def _():
+            attend(back, qb)
+
+        finish(qb)
+        a_copy(qb).start()
+
+        @pl.when(k >= 1)
+        def _():
+            multiply(0, qb + 1)
+
+        @pl.when((k >= 2) & (kept == 0))
+        def _():
+            combine(qb + 2)
+
+        return carry
+
+    lax.fori_loop(0, inner, finish_rows, 0)
+    multiply(0, 0)
+
+    @pl.when(kept == 0)
+    def _():
+        combine(1)
+        combine(0)
+        first_sums()
+
+    for d in range(inner):
+        slot = w_all.at[1, from_mate(d)]
+        remote(slot, slot, f_send.at[d], f_recv.at[d], far).wait_recv()
+
+    def far_rows(k, carry):
+        qb = inner - 1 - k
+
+        @pl.when(k < inner)
+        def _():
+            multiply(1, qb)
+
+        @pl.when((k >= 1) & (kept == 1))
+        def _():
+            combine(qb + 1)
+
+        return carry
+
+    lax.fori_loop(0, inner + 1, far_rows, 0)
+
+    @pl.when(kept == 1)
+    def _():
+        first_sums()
+
+    for c in range(2):
+        second_sum(c)
+    for c in range(2):
+        slot = final_in.at[c]
+        remote(slot, slot, o_send.at[c], o_recv.at[c], pair).wait_recv()
+        out_ref[:, columns(1 - low, c)] = final_in[c]
+
+    for d in range(1, inner):
+        for copy in kv_copies(d):
+            copy.wait_send()
+        q_copy(d).wait_send()
+        w_copy(d).wait_send()
+    for d in range(inner):
+        far_copy(d).wait_send()
+    for b in range(back):
+        @pl.when(has_above & (o >= b))
+        def _():
+            for copy in lift(b):
+                copy.wait_send()
+    for qb in range(inner):
+        a_copy(qb).wait_send()
+        give(qb, 1 - kept).wait_send()
+        for c in range(2):
+            @pl.when(is_sent(qb, c))
+            def _():
+                first_copy(qb, c).wait_send()
+    for c in range(2):
+        second_copy(c, 1 - (iy if c == 0 else ix)).wait_send()
+        out_copy(c).wait_send()
+
+
+def paired_scratch(inner, heads, group, back, tok, width, wide):
+    bf16, f32 = jnp.bfloat16, jnp.float32
+    dma = pltpu.SemaphoreType.DMA
+    half = (inner // 2) * wide
+    scratch = [
+        pltpu.VMEM((inner, width, group * tok), bf16),
+        pltpu.VMEM((inner, tok, width), bf16),
+        pltpu.VMEM((inner, width, tok), bf16),
+        pltpu.VMEM((inner, width, group * tok), bf16),
+        pltpu.VMEM((back + 1, inner, tok, width), bf16),
+        pltpu.VMEM((back + 1, inner, width, tok), bf16),
+        pltpu.VMEM((2, inner, group * width, wide), bf16),
+        pltpu.VMEM((2, inner, tok, group * width), bf16),
+        pltpu.VMEM((inner, width, group * tok), f32),
+        pltpu.VMEM((inner, 1, group * tok), f32),
+        pltpu.VMEM((inner, 1, group * tok), f32),
+        pltpu.VMEM((2, inner, 2, 2, tok, half), bf16),
+        pltpu.VMEM((inner, 2, 2, tok, half), bf16),
+        pltpu.VMEM((2, 2, 2, tok, half), bf16),
+        pltpu.VMEM((2, 2, tok, half), bf16),
+        pltpu.VMEM((2, tok, half), bf16),
+        pltpu.VMEM((2, tok, half), bf16),
+    ]
+    scratch += [dma((inner,))] * 6 + [dma((back + 1,))] * 4 + [dma((inner,))] * 8
+    return scratch + [dma((2, 2))] * 2 + [dma((2,))] * 4 + [dma((4,))]
 
 
 def body(queries, keys, values, out_weight, doc_lengths):
@@ -519,8 +937,11 @@
     scratch += [dma((inner,))] * 6 + [dma((back + 1,))] * 4 + [dma((outer,))] * 4
     scratch += [dma((inner, inner))] * 2 + [dma((outer,)), dma((heads, share))] + [dma((share, inner))] * 2 + [dma((4,))]
     shape = (inner, outer, heads, group, back, span, last)
+    run = kernel
+    if inner == 4 and outer == 4 and heads == 2 and back > 2:
+        run, scratch = paired_kernel, paired_scratch(inner, heads, group, back, tok, width, wide)
     return pl.pallas_call(
-        functools.partial(kernel, shape),
+        functools.partial(run, shape),
         out_shape=jax.ShapeDtypeStruct((tok, share * inner * wide), bf16),
         in_specs=[pl.BlockSpec(memory_space=pltpu.VMEM)] * 5,
         out_specs=pl.BlockSpec(memory_space=pltpu.VMEM),

time: 120 us -> 150 us (1.25)
  Pallas kernels: 116 us -> 146 us
    pallas_call x1, Pallas kernels: 116 us -> 146 us  [body(): pl.pallas_call(functools.partial(run, shape), out_shape=jax.ShapeDtypeStr...]
where the time goes in v1:
time: 150 us
  Pallas kernels  146 us (97%)
  local copies, waits for them, and re-layouts  3.04 us (2%)
    pallas_call x1, Pallas kernels, body(): pl.pallas_call(functools.partial(run, shape), out_shape=jax.ShapeDtypeStr...  146 us

profile of v1, /device:TPU:24, one launch (start us, length us, event | category | flops | bytes accessed | tf_op | source)
XLA Modules:
  0.0 149.8 jit_solution(18406275273680264009)
XLA Ops:
  0.0 0.0 copy-start
  0.0 0.6 copy-done
  0.7 0.1 copy.8
  0.8 0.1 reduce
  0.9 0.7 select_reduce_fusion
  1.6 145.9 %shard_map.55 = bf16[256,2048]{1,0:T(8,128)(2,1)} custom-call(bf16[256,16,128]{2,1,0:T(8,128)(2,1)} %q_in.1, bf16[256,4,128]{2,1,0:T(4,128)(2,1)} %k_in.1, bf16[256,4,128]{2,1,0:T(4,128)(2,1)} %v_in.1, bf16[2048,256]{1,0:T(8,128)(2,1)} %w_ref.1, s32[4,1,256]{2,1,0:T(1,128)} %bitcast.2), custom_call_target="tpu_custom_call" | custom-call | tf_op jit(solution)/shard_map/pallas_call | solution.py:943
  147.5 2.3 %copy.10 = bf16[256,2048]{1,0:T(8,128)(2,1)} copy(bf16[256,2048]{1,0:T(8,128)(2,1)} %shard_map.55) | data formatting | bytes 2097152
  (2 shorter events, 0.0 us)
Async XLA Ops:
  0.0 0.7 copy-start

commit v2 on v0

--- a/solution.py
+++ b/solution.py
@@ -171,10 +171,13 @@
                 jnp.int32, (tok, tok), 1
             )
         keys_here, values_here = k_all[b, kb], v_all[b, kb]
+        raw = [
+            jnp.dot(keys_here, q_all[qb, :, r * tok : (r + 1) * tok], preferred_element_type=jnp.float32)
+            for r in range(group)
+        ]
         for r in range(group):
             cols = pl.ds(r * tok, tok)
-            scores = jnp.dot(keys_here, q_all[qb, :, cols], preferred_element_type=jnp.float32)
-            scores = jnp.where(allowed, scores * factor, -1e30)
+            scores = jnp.where(allowed, raw[r] * factor, -1e30)
             old_max = row_max[qb, :, cols]
             new_max = jnp.maximum(old_max, jnp.max(scores, axis=0, keepdims=True))
             weights = jnp.exp2(scores - new_max)
@@ -475,6 +478,503 @@
     if outer > 1:
         hop_sent(1, True)
         lax.fori_loop(2, outer, later_sent, 0)
+
+
+def square_kernel(
+    shape,
+    q_in, k_in, v_in, w_ref, doc_ref, out_ref,
+    lo_ref,
+    q_ref, k_ref, v_ref,
+    q_all, k_all, v_all, w_all, a_all, acc, row_max, row_total, partial, peer, summed, result,
+    q_send, q_recv, k_send, k_recv, v_send, v_recv, kz_send, kz_recv, vz_send, vz_recv,
+    up_send, up_recv, down_send, down_recv, a_send, a_recv, g_send, g_recv, p_send, p_recv, c_send, c_recv,
+    hp_send, hp_recv, hc_send, hc_recv, local_sem,
+):
+    inner, outer, heads, group, back, span, last = shape
+    tok, width = k_in.shape[0], k_in.shape[2]
+    part_rows = group * width
+    share = outer // heads
+    seq, head = lax.axis_index("seq"), lax.axis_index("head")
+    o, i = seq // inner, seq % inner
+    ix, iy = i % 2, i // 2
+    near_x, near_y = iy * 2 + 1 - ix, (1 - iy) * 2 + ix
+    half = w_ref.shape[1] // 2
+
+    def remote(src, dst, send, recv, device):
+        return pltpu.make_async_remote_copy(
+            src_ref=src, dst_ref=dst, send_sem=send, recv_sem=recv, device_id=device, device_id_type=MESH
+        )
+
+    def mate(d):
+        return (i + d) % inner
+
+    def plane(d):
+        return {"seq": o * inner + mate(d)}
+
+    above, below = {"seq": jnp.minimum(seq + inner, outer * inner - 1)}, {"seq": jnp.maximum(seq - inner, 0)}
+    has_above, has_below = o + 1 < outer, o >= 1
+
+    barrier = pltpu.get_barrier_semaphore()
+    for d in range(1, inner):
+        pl.semaphore_signal(barrier, inc=1, device_id=plane(d), device_id_type=MESH)
+    for d in range(1, heads):
+        pl.semaphore_signal(barrier, inc=1, device_id={"head": (head + d) % heads}, device_id_type=MESH)
+
+    @pl.when(has_above)
+    def _():
+        pl.semaphore_signal(barrier, inc=1, device_id=above, device_id_type=MESH)
+
+    @pl.when(has_below)
+    def _():
+        pl.semaphore_signal(barrier, inc=1, device_id=below, device_id_type=MESH)
+
+    pl.semaphore_wait(
+        barrier, inner - 1 + heads - 1 + has_above.astype(jnp.int32) + has_below.astype(jnp.int32)
+    )
+
+    def kv_copies(d):
+        return (
+            remote(k_ref.at[mate(d)], k_all.at[0, i], k_send.at[d], k_recv.at[d], plane(d)),
+            remote(v_ref.at[mate(d)], v_all.at[0, i], v_send.at[d], v_recv.at[d], plane(d)),
+        )
+
+    def q_copy(d):
+        return remote(q_ref.at[mate(d)], q_all.at[i], q_send.at[d], q_recv.at[d], plane(d))
+
+    def slot_up(t, c):
+        return w_all.at[jnp.maximum(o - t, 0), :, pl.ds(c * half, half)]
+
+    def slot_down(t, c):
+        return w_all.at[jnp.minimum(o + t, outer - 1), :, pl.ds(c * half, half)]
+
+    def up_copy(t, c):
+        src = w_ref.at[:, pl.ds(c * half, half)] if t == 1 else slot_up(t - 1, c)
+        return remote(src, slot_up(t - 1, c), up_send.at[t, c], up_recv.at[t, c], above)
+
+    def down_copy(t, c):
+        src = w_ref.at[:, pl.ds(c * half, half)] if t == 1 else slot_down(t - 1, c)
+        return remote(src, slot_down(t - 1, c), down_send.at[t, c], down_recv.at[t, c], below)
+
+    def got_up(t, c):
+        @pl.when(o >= t)
+        def _():
+            remote(slot_up(t, c), slot_up(t, c), up_send.at[t, c], up_recv.at[t, c], below).wait_recv()
+
+    def got_down(t, c):
+        @pl.when(o + t < outer)
+        def _():
+            remote(slot_down(t, c), slot_down(t, c), down_send.at[t, c], down_recv.at[t, c], above).wait_recv()
+
+    def go_up(t, c):
+        @pl.when(has_above & (o >= t - 1))
+        def _():
+            up_copy(t, c).start()
+
+    def go_down(t, c):
+        @pl.when(has_below & (o + t - 1 < outer))
+        def _():
+            down_copy(t, c).start()
+
+    def pass_up(t, c):
+        got_up(t, c)
+        go_up(t + 1, c)
+
+    def pass_down(t, c):
+        got_down(t, c)
+        go_down(t + 1, c)
+
+    if outer > 1:
+        go_up(1, 0)
+        go_down(1, 0)
+        go_down(1, 1)
+    k_ref[...] = jnp.swapaxes(k_in[...], 0, 1)
+    by_head = jnp.swapaxes(v_in[...], 0, 1)
+    for j in range(inner):
+        v_ref[j] = by_head[j].T
+    by_head = jnp.swapaxes(q_in[...], 0, 1)
+    for j in range(inner * group):
+        q_ref[j // group, :, (j % group) * tok : (j % group + 1) * tok] = by_head[j].T
+    for d in range(1, inner):
+        for copy in kv_copies(d):
+            copy.start()
+    for d in range(1, inner):
+        q_copy(d).start()
+
+    locals_ = [
+        pltpu.make_async_copy(q_ref.at[i], q_all.at[i], local_sem.at[0]),
+        pltpu.make_async_copy(k_ref.at[i], k_all.at[0, i], local_sem.at[1]),
+        pltpu.make_async_copy(v_ref.at[i], v_all.at[0, i], local_sem.at[2]),
+        pltpu.make_async_copy(w_ref, w_all.at[o], local_sem.at[3]),
+    ]
+    for copy in locals_:
+        copy.start()
+    row_max[...] = jnp.full(row_max.shape, -1e30, jnp.float32)
+    row_total[...] = jnp.zeros(row_total.shape, jnp.float32)
+    acc[...] = jnp.zeros(acc.shape, jnp.float32)
+    ends = [doc_ref[0]]
+    for j in range(1, doc_ref.shape[0]):
+        ends.append(ends[-1] + doc_ref[j])
+    for qb in range(inner):
+        row = (o * inner + qb) * tok + lax.broadcasted_iota(jnp.int32, (1, tok), 1)
+        start = jnp.zeros((1, tok), jnp.int32)
+        for end in ends:
+            start = jnp.where(row >= end, end, start)
+        lo_ref[qb] = start
+    for copy in locals_:
+        copy.wait()
+
+    def from_mate(d):
+        return (i + inner - d) % inner
+
+    for d in range(1, inner):
+        k_slot, v_slot = k_all.at[0, from_mate(d)], v_all.at[0, from_mate(d)]
+        remote(k_slot, k_slot, k_send.at[d], k_recv.at[d], plane(d)).wait_recv()
+        remote(v_slot, v_slot, v_send.at[d], v_recv.at[d], plane(d)).wait_recv()
+
+    def slot_of(ref, b, only_last):
+        return ref.at[b, pl.ds(inner - last, last)] if only_last else ref.at[b]
+
+    def lift(b, only_last):
+        return (
+            remote(slot_of(k_all, b, only_last), slot_of(k_all, b + 1, only_last), kz_send.at[b], kz_recv.at[b + 1], above),
+            remote(slot_of(v_all, b, only_last), slot_of(v_all, b + 1, only_last), vz_send.at[b], vz_recv.at[b + 1], above),
+        )
+
+    def start_lift(b, only_last):
+        @pl.when(has_above & (o >= b))
+        def _():
+            for copy in lift(b, only_last):
+                copy.start()
+
+    def got_lift(b, only_last):
+        k_slot, v_slot = slot_of(k_all, b, only_last), slot_of(v_all, b, only_last)
+        remote(k_slot, k_slot, kz_send.at[b], kz_recv.at[b], below).wait_recv()
+        remote(v_slot, v_slot, vz_send.at[b], vz_recv.at[b], below).wait_recv()
+
+    if back >= 1:
+        start_lift(0, back == 1)
+    factor = math.log2(math.e) / math.sqrt(width)
+
+    def tile(b, qb, kb, diagonal):
+        key_pos = ((o - b) * inner + kb) * tok + lax.broadcasted_iota(jnp.int32, (tok, tok), 0)
+        allowed = key_pos >= lo_ref[qb]
+        if diagonal:
+            allowed &= lax.broadcasted_iota(jnp.int32, (tok, tok), 0) <= lax.broadcasted_iota(
+                jnp.int32, (tok, tok), 1
+            )
+        keys_here, values_here = k_all[b, kb], v_all[b, kb]
+        raw = [
+            jnp.dot(keys_here, q_all[qb, :, r * tok : (r + 1) * tok], preferred_element_type=jnp.float32)
+            for r in range(group)
+        ]
+        for r in range(group):
+            cols = pl.ds(r * tok, tok)
+            scores = jnp.where(allowed, raw[r] * factor, -1e30)
+            old_max = row_max[qb, :, cols]
+            new_max = jnp.maximum(old_max, jnp.max(scores, axis=0, keepdims=True))
+            weights = jnp.exp2(scores - new_max)
+            rescale = jnp.exp2(old_max - new_max)
+            row_max[qb, :, cols] = new_max
+            row_total[qb, :, cols] = row_total[qb, :, cols] * rescale + jnp.sum(weights, axis=0, keepdims=True)
+            acc[qb, :, cols] = acc[qb, :, cols] * rescale + jnp.dot(
+                values_here, weights.astype(jnp.bfloat16), preferred_element_type=jnp.float32
+            )
+
+    def own_rows(qb, carry):
+        tile(0, qb, qb, True)
+
+        def own_keys(kb, inside):
+            tile(0, qb, kb, False)
+            return inside
+
+        return lax.fori_loop(0, qb, own_keys, carry)
+
+    own_rows(i, 0)
+
+    @pl.when(o >= 1)
+    def _():
+        got_lift(1, False)
+
+    start_lift(1, False)
+    go_up(1, 1)
+    for d in range(1, inner):
+        q_slot = q_all.at[from_mate(d)]
+        remote(q_slot, q_slot, q_send.at[d], q_recv.at[d], plane(d)).wait_recv()
+        own_rows(from_mate(d), 0)
+    for c in range(2):
+        pass_down(1, c)
+    pass_up(1, 0)
+
+    def attend(b, qb):
+        def cols(kb, inside):
+            tile(b, qb, kb, False)
+            return inside
+
+        lax.fori_loop(jnp.maximum(b * inner + qb - span, 0), inner, cols, 0)
+
+    def early_rows(k, carry):
+        attend(1, inner - 1 - k)
+        return carry
+
+    @pl.when(o >= 1)
+    def _():
+        lax.fori_loop(0, inner, early_rows, 0)
+
+    @pl.when(o >= 2)
+    def _():
+        got_lift(2, False)
+
+    start_lift(2, True)
+    pass_up(1, 1)
+
+    def a_copy(qb, k):
+        slot = a_all.at[qb, i]
+        to = {"seq": o * inner + (near_x if k == 0 else near_y)}
+        return remote(slot, slot, a_send.at[qb, k], a_recv.at[qb, k], to)
+
+    def send_rows(qb):
+        for k in range(2):
+            a_copy(qb, k).start()
+
+    def got_near(qb, k):
+        slot = a_all.at[qb, near_x if k == 0 else near_y]
+        remote(slot, slot, a_send.at[qb, k], a_recv.at[qb, k], plane(1)).wait_recv()
+
+    def relay(qb, k):
+        slot = a_all.at[qb, near_x if k == 0 else near_y, pl.ds(k * (tok // 2), tok // 2)]
+        to = {"seq": o * inner + (near_y if k == 0 else near_x)}
+        return remote(slot, slot, g_send.at[qb, k], g_recv.at[qb, k], to)
+
+    def got_rows(qb):
+        for k in range(2):
+            slot = a_all.at[qb, inner - 1 - i, pl.ds(k * (tok // 2), tok // 2)]
+            remote(slot, slot, g_send.at[qb, k], g_recv.at[qb, k], plane(1)).wait_recv()
+
+    def finish(qb):
+        for r in range(group):
+            cols = pl.ds(r * tok, tok)
+            normal = acc[qb, :, cols] / row_total[qb, :, cols]
+            a_all[qb, i, :, r * width : (r + 1) * width] = normal.T.astype(jnp.bfloat16)
+
+    deepest = min(inner, span + inner - back * inner)
+
+    def finish_rows(k, carry):
+        qb = inner - 1 - k
+
+        def slots(b, inside):
+            attend(b, qb)
+            return inside
+
+        lax.fori_loop(2, jnp.minimum(o, back - 1) + 1, slots, 0)
+        if back > 1:
+            @pl.when((o >= back) & (qb == deepest - 1))
+            def _():
+                got_lift(back, True)
+
+        if back >= 1:
+            @pl.when((o >= back) & (qb < deepest))
+            def _():
+                attend(back, qb)
+
+        finish(qb)
+        send_rows(qb)
+        return carry
+
+    lax.fori_loop(0, inner, finish_rows, 0)
+
+    def pass_rows(qb):
+        for k in range(2):
+            got_near(qb, k)
+            relay(qb, k).start()
+
+    pass_rows(inner - 1)
+    for c in range(2):
+        pass_down(2, c)
+    pass_up(2, 0)
+    for qb in range(inner - 2, -1, -1):
+        pass_rows(qb)
+    pass_up(2, 1)
+
+    def multiply(qb, s, cols=slice(None)):
+        value = jnp.dot(a_all[qb, 0], w_all[s, 0:part_rows, cols], preferred_element_type=jnp.float32)
+        for j in range(1, inner):
+            value += jnp.dot(
+                a_all[qb, j], w_all[s, j * part_rows : (j + 1) * part_rows, cols], preferred_element_type=jnp.float32
+            )
+        partial[s, qb, :, cols] = value.astype(jnp.bfloat16)
+
+    def columns(c):
+        return pl.ds(0, 2 * half) if c is None else pl.ds(c * half, half)
+
+    def p_copy(s, c=None):
+        to = s // share
+        d = (to + heads - head) % heads
+        sl = s % share
+        src, dst = partial.at[s, :, :, columns(c)], peer.at[d, sl, :, :, columns(c)]
+        if c is None:
+            return remote(src, dst, p_send.at[s], p_recv.at[d, sl], {"head": to})
+        return remote(src, dst, hp_send.at[c], hp_recv.at[c], {"head": to})
+
+    def give(s, c=None):
+        @pl.when(s // share != head)
+        def _():
+            p_copy(s, c).start()
+
+    def c_copy(sl, d, c=None):
+        src, dst = summed.at[sl, mate(d), :, columns(c)], result.at[sl, i, :, columns(c)]
+        if c is None:
+            return remote(src, dst, c_send.at[sl, d], c_recv.at[sl, d], plane(d))
+        return remote(src, dst, hc_send.at[c, d], hc_recv.at[c, d], plane(d))
+
+    def absorb(s, c=None):
+        @pl.when(s // share == head)
+        def _():
+            sl = s % share
+            cols = columns(c)
+            for d in range(1, heads):
+                slot = peer.at[d, sl, :, :, cols]
+                if c is None:
+                    arrived = p_recv.at[d, sl]
+                else:
+                    arrived = hp_recv.at[c]
+                remote(slot, slot, p_send.at[s], arrived, {"head": (head + d) % heads}).wait_recv()
+
+            def rows(j, carry):
+                total = partial[s, j, :, cols].astype(jnp.float32)
+                for d in range(1, heads):
+                    total = total + peer[d, sl, j, :, cols].astype(jnp.float32)
+                summed[sl, j, :, cols] = total.astype(jnp.bfloat16)
+                return carry
+
+            lax.fori_loop(0, inner, rows, 0)
+            for d in range(1, inner):
+                c_copy(sl, d, c).start()
+            result[sl, i, :, cols] = summed[sl, i, :, cols]
+
+    def near(t, act):
+        @pl.when(o - t >= 0)
+        def _():
+            act(jnp.maximum(o - t, 0))
+
+        @pl.when((o + t < outer) & (t > 0))
+        def _():
+            act(jnp.minimum(o + t, outer - 1))
+
+    near_count = max(outer - 1, 1)
+
+    def early_blocks(k, carry):
+        qb = inner - 1 - k
+        got_rows(qb)
+
+        def shards(t, inside):
+            near(t, lambda s: multiply(qb, s))
+            return inside
+
+        lax.fori_loop(0, near_count, shards, 0)
+        return carry
+
+    lax.fori_loop(0, inner - 1, early_blocks, 0)
+    got_rows(0)
+
+    def final_block(t, carry):
+        def act(s):
+            multiply(0, s)
+            give(s)
+
+        near(t, act)
+
+        @pl.when(t >= 1)
+        def _():
+            near(t - 1, absorb)
+
+        return carry
+
+    lax.fori_loop(0, near_count, final_block, 0)
+    near(near_count - 1, absorb)
+    for c in range(2):
+        got_down(outer - 1, c)
+        got_up(outer - 1, c)
+
+        def far(s):
+            def rows(qb, carry):
+                multiply(qb, s, pl.ds(c * half, half))
+                return carry
+
+            lax.fori_loop(0, inner, rows, 0)
+            give(s, c)
+
+        near(outer - 1, far)
+        near(outer - 1, lambda s: absorb(s, c))
+
+    def is_far(s):
+        return (s - o == outer - 1) | (o - s == outer - 1)
+
+    for sl in range(share):
+        for d in range(1, inner):
+            @pl.when(is_far(head * share + sl))
+            def _():
+                for c in range(2):
+                    slot = result.at[sl, from_mate(d), :, columns(c)]
+                    remote(slot, slot, hc_send.at[c, d], hc_recv.at[c, d], plane(d)).wait_recv()
+
+            @pl.when(jnp.logical_not(is_far(head * share + sl)))
+            def _():
+                slot = result.at[sl, from_mate(d)]
+                remote(slot, slot, c_send.at[sl, d], c_recv.at[sl, d], plane(d)).wait_recv()
+
+    wide = out_ref.shape[1] // (share * inner)
+    for s in range(share):
+        for j in range(inner):
+            out_ref[:, (s * inner + j) * wide : (s * inner + j + 1) * wide] = result[s, j]
+
+    for d in range(1, inner):
+        for copy in kv_copies(d):
+            copy.wait_send()
+        q_copy(d).wait_send()
+        for sl in range(share):
+            @pl.when(is_far(head * share + sl))
+            def _():
+                for c in range(2):
+                    c_copy(sl, d, c).wait_send()
+
+            @pl.when(jnp.logical_not(is_far(head * share + sl)))
+            def _():
+                c_copy(sl, d).wait_send()
+
+    for qb in range(inner):
+        for k in range(2):
+            a_copy(qb, k).wait_send()
+            relay(qb, k).wait_send()
+
+    def given(s, carry):
+        @pl.when((s // share != head) & is_far(s))
+        def _():
+            for c in range(2):
+                p_copy(s, c).wait_send()
+
+        @pl.when((s // share != head) & jnp.logical_not(is_far(s)))
+        def _():
+            p_copy(s).wait_send()
+
+        return carry
+
+    lax.fori_loop(0, outer, given, 0)
+
+    for b in range(back):
+        @pl.when(has_above & (o >= b))
+        def _():
+            for copy in lift(b, b == back - 1):
+                copy.wait_send()
+
+    for t in range(1, outer):
+        for c in range(2):
+            @pl.when(has_above & (o >= t - 1))
+            def _():
+                up_copy(t, c).wait_send()
+
+            @pl.when(has_below & (o + t - 1 < outer))
+            def _():
+                down_copy(t, c).wait_send()
 
 
 def body(queries, keys, values, out_weight, doc_lengths):
@@ -519,16 +1019,24 @@
     scratch += [dma((inner,))] * 6 + [dma((back + 1,))] * 4 + [dma((outer,))] * 4
     scratch += [dma((inner, inner))] * 2 + [dma((outer,)), dma((heads, share))] + [dma((share, inner))] * 2 + [dma((4,))]
     shape = (inner, outer, heads, group, back, span, last)
+    vmem = pl.BlockSpec(memory_space=pltpu.VMEM)
+    run, last_in, last_spec = kernel, starts, vmem
+    if inner == 4 and outer == 4 and back == 3:
+        run, last_in, last_spec = square_kernel, doc_lengths, pl.BlockSpec(memory_space=pltpu.SMEM)
+        scratch = [pltpu.VMEM((inner, 1, tok), jnp.int32)] + scratch[:15]
+        scratch += [dma((inner,))] * 6 + [dma((back + 1,))] * 4 + [dma((outer, 2))] * 4
+        scratch += [dma((inner, 2))] * 4 + [dma((outer,)), dma((heads, share))] + [dma((share, inner))] * 2
+        scratch += [dma((2,))] * 2 + [dma((2, inner))] * 2 + [dma((4,))]
     return pl.pallas_call(
-        functools.partial(kernel, shape),
+        functools.partial(run, shape),
         out_shape=jax.ShapeDtypeStruct((tok, share * inner * wide), bf16),
-        in_specs=[pl.BlockSpec(memory_space=pltpu.VMEM)] * 5,
-        out_specs=pl.BlockSpec(memory_space=pltpu.VMEM),
+        in_specs=[vmem] * 4 + [last_spec],
+        out_specs=vmem,
         scratch_shapes=scratch,
         compiler_params=pltpu.CompilerParams(
             collective_id=0, has_side_effects=True, vmem_limit_bytes=60 * 1024 * 1024
         ),
-    )(queries, keys, values, out_weight, starts)
+    )(queries, keys, values, out_weight, last_in)
 
 
 def solution(mesh):

time: 120 us -> 109 us (0.908)
  Pallas kernels: 116 us -> 106 us
    pallas_call x1, Pallas kernels: 116 us -> 106 us  [body(): pl.pallas_call(functools.partial(run, shape), out_shape=jax.ShapeDtypeStr...]
    unnamed x3 -> x1, local copies, waits for them, and re-layouts: 2.96 us -> 2.3 us
where the time goes in v2:
time: 109 us
  Pallas kernels  106 us (97%)
  local copies, waits for them, and re-layouts  2.3 us (2%)
    pallas_call x1, Pallas kernels, body(): pl.pallas_call(functools.partial(run, shape), out_shape=jax.ShapeDtypeStr...  106 us
    unnamed x1, local copies, waits for them, and re-layouts  2.3 us

profile of v2, /device:TPU:24, one launch (start us, length us, event | category | flops | bytes accessed | tf_op | source)
XLA Modules:
  0.0 108.6 jit_solution(17064713508252232107)
XLA Ops:
  0.0 106.3 %shard_map.55 = bf16[256,2048]{1,0:T(8,128)(2,1)} custom-call(bf16[256,16,128]{2,1,0:T(8,128)(2,1)} %q_in.1, bf16[256,4,128]{2,1,0:T(4,128)(2,1)} %k_in.1, bf16[256,4,128]{2,1,0:T(4,128)(2,1)} %v_in.1, bf16[2048,256]{1,0:T(8,128)(2,1)} %w_ref.1, s32[16]{0:T(128)} %doc_ref.1), custom_call_target="tpu_custom_call" | custom-call | tf_op jit(solution)/shard_map/pallas_call | solution.py:1030
  106.3 2.3 %copy.7 = bf16[256,2048]{1,0:T(8,128)(2,1)} copy(bf16[256,2048]{1,0:T(8,128)(2,1)} %shard_map.55) | data formatting | bytes 2097152

commit v3 on v2

--- a/solution.py
+++ b/solution.py
@@ -482,13 +482,13 @@
 
 def square_kernel(
     shape,
-    q_in, k_in, v_in, w_ref, doc_ref, out_ref,
-    lo_ref,
+    q_hbm, k_hbm, v_hbm, w_hbm, doc_ref, out_ref,
+    q_in, k_in, v_in, w_ref, lo_ref,
     q_ref, k_ref, v_ref,
     q_all, k_all, v_all, w_all, a_all, acc, row_max, row_total, partial, peer, summed, result,
     q_send, q_recv, k_send, k_recv, v_send, v_recv, kz_send, kz_recv, vz_send, vz_recv,
     up_send, up_recv, down_send, down_recv, a_send, a_recv, g_send, g_recv, p_send, p_recv, c_send, c_recv,
-    hp_send, hp_recv, hc_send, hc_recv, local_sem,
+    hp_send, hp_recv, hc_send, hc_recv, in_sem, local_sem,
 ):
     inner, outer, heads, group, back, span, last = shape
     tok, width = k_in.shape[0], k_in.shape[2]
@@ -514,6 +514,13 @@
     above, below = {"seq": jnp.minimum(seq + inner, outer * inner - 1)}, {"seq": jnp.maximum(seq - inner, 0)}
     has_above, has_below = o + 1 < outer, o >= 1
 
+    fetch_w, fetch_k, fetch_v, fetch_q = (
+        pltpu.make_async_copy(src, dst, in_sem.at[j])
+        for j, (src, dst) in enumerate(((w_hbm, w_ref), (k_hbm, k_in), (v_hbm, v_in), (q_hbm, q_in)))
+    )
+    for fetch in (fetch_w, fetch_k, fetch_v, fetch_q):
+        fetch.start()
+
     barrier = pltpu.get_barrier_semaphore()
     for d in range(1, inner):
         pl.semaphore_signal(barrier, inc=1, device_id=plane(d), device_id_type=MESH)
@@ -584,19 +591,23 @@
         go_down(t + 1, c)
 
     if outer > 1:
+        fetch_w.wait()
         go_up(1, 0)
         go_down(1, 0)
         go_down(1, 1)
+    fetch_k.wait()
     k_ref[...] = jnp.swapaxes(k_in[...], 0, 1)
+    fetch_v.wait()
     by_head = jnp.swapaxes(v_in[...], 0, 1)
     for j in range(inner):
         v_ref[j] = by_head[j].T
+    for d in range(1, inner):
+        for copy in kv_copies(d):
+            copy.start()
+    fetch_q.wait()
     by_head = jnp.swapaxes(q_in[...], 0, 1)
     for j in range(inner * group):
         q_ref[j // group, :, (j % group) * tok : (j % group + 1) * tok] = by_head[j].T
-    for d in range(1, inner):
-        for copy in kv_copies(d):
-            copy.start()
     for d in range(1, inner):
         q_copy(d).start()
 
@@ -806,50 +817,77 @@
     def columns(c):
         return pl.ds(0, 2 * half) if c is None else pl.ds(c * half, half)
 
-    def p_copy(s, c=None):
+    def p_copy(s):
         to = s // share
         d = (to + heads - head) % heads
-        sl = s % share
-        src, dst = partial.at[s, :, :, columns(c)], peer.at[d, sl, :, :, columns(c)]
-        if c is None:
-            return remote(src, dst, p_send.at[s], p_recv.at[d, sl], {"head": to})
-        return remote(src, dst, hp_send.at[c], hp_recv.at[c], {"head": to})
-
-    def give(s, c=None):
+        return remote(
+            partial.at[s], peer.at[d, s % share], p_send.at[s], p_recv.at[d, s % share], {"head": to}
+        )
+
+    def give(s):
         @pl.when(s // share != head)
         def _():
-            p_copy(s, c).start()
-
-    def c_copy(sl, d, c=None):
-        src, dst = summed.at[sl, mate(d), :, columns(c)], result.at[sl, i, :, columns(c)]
-        if c is None:
-            return remote(src, dst, c_send.at[sl, d], c_recv.at[sl, d], plane(d))
-        return remote(src, dst, hc_send.at[c, d], hc_recv.at[c, d], plane(d))
-
-    def absorb(s, c=None):
+            p_copy(s).start()
+
+    def c_copy(sl, d):
+        return remote(summed.at[sl, mate(d)], result.at[sl, i], c_send.at[sl, d], c_recv.at[sl, d], plane(d))
+
+    def absorb(s):
         @pl.when(s // share == head)
         def _():
             sl = s % share
-            cols = columns(c)
             for d in range(1, heads):
-                slot = peer.at[d, sl, :, :, cols]
-                if c is None:
-                    arrived = p_recv.at[d, sl]
-                else:
-                    arrived = hp_recv.at[c]
-                remote(slot, slot, p_send.at[s], arrived, {"head": (head + d) % heads}).wait_recv()
+                slot = peer.at[d, sl]
+                remote(slot, slot, p_send.at[s], p_recv.at[d, sl], {"head": (head + d) % heads}).wait_recv()
 
             def rows(j, carry):
-                total = partial[s, j, :, cols].astype(jnp.float32)
+                total = partial[s, j].astype(jnp.float32)
                 for d in range(1, heads):
-                    total = total + peer[d, sl, j, :, cols].astype(jnp.float32)
-                summed[sl, j, :, cols] = total.astype(jnp.bfloat16)
+                    total = total + peer[d, sl, j].astype(jnp.float32)
+                summed[sl, j] = total.astype(jnp.bfloat16)
                 return carry
 
             lax.fori_loop(0, inner, rows, 0)
             for d in range(1, inner):
-                c_copy(sl, d, c).start()
-            result[sl, i, :, cols] = summed[sl, i, :, cols]
+                c_copy(sl, d).start()
+            result[sl, i] = summed[sl, i]
+
+    def block(k):
+        return jnp.where(k == 0, inner - 1 - i, jnp.where(k == 1, near_x, jnp.where(k == 2, near_y, i)))
+
+    def far_give(s, c, k):
+        to = s // share
+        d = (to + heads - head) % heads
+        cols = columns(c)
+        return remote(
+            partial.at[s, block(k), :, cols], peer.at[d, s % share, block(k), :, cols],
+            hp_send.at[c, k], hp_recv.at[c, k], {"head": to},
+        )
+
+    def far_copy(s, c, k):
+        sl, cols = s % share, columns(c)
+        return remote(
+            summed.at[sl, block(k), :, cols], result.at[sl, i, :, cols],
+            hc_send.at[c, k], hc_recv.at[c, k], {"seq": o * inner + block(k)},
+        )
+
+    def far_absorb(s, c, k):
+        sl, cols, qb = s % share, columns(c), block(k)
+        total = partial[s, qb, :, cols].astype(jnp.float32)
+        for d in range(1, heads):
+            slot = peer.at[d, sl, qb, :, cols]
+            remote(slot, slot, hp_send.at[c, k], hp_recv.at[c, k], {"head": (head + d) % heads}).wait_recv()
+            total = total + peer[d, sl, qb, :, cols].astype(jnp.float32)
+        total = total.astype(jnp.bfloat16)
+
+        @pl.when(k < inner - 1)
+        def _():
+            summed[sl, qb, :, cols] = total
+            far_copy(s, c, k).start()
+
+        @pl.when(k == inner - 1)
+        def _():
+            result[sl, i, :, cols] = total
 
     def near(t, act):
         @pl.when(o - t >= 0)
@@ -896,29 +934,39 @@
         got_up(outer - 1, c)
 
         def far(s):
-            def rows(qb, carry):
-                multiply(qb, s, pl.ds(c * half, half))
+            def rows(k, carry):
+                @pl.when(k < inner)
+                def _():
+                    multiply(block(k), s, columns(c))
+
+                @pl.when((k < inner) & (s // share != head))
+                def _():
+                    far_give(s, c, k).start()
+
+                @pl.when((k >= 1) & (s // share == head))
+                def _():
+                    far_absorb(s, c, k - 1)
+
                 return carry
 
-            lax.fori_loop(0, inner, rows, 0)
-            give(s, c)
+            lax.fori_loop(0, inner + 1, rows, 0)
 
         near(outer - 1, far)
-        near(outer - 1, lambda s: absorb(s, c))
 
     def is_far(s):
         return (s - o == outer - 1) | (o - s == outer - 1)
 
     for sl in range(share):
-        for d in range(1, inner):
-            @pl.when(is_far(head * share + sl))
-            def _():
-                for c in range(2):
-                    slot = result.at[sl, from_mate(d), :, columns(c)]
-                    remote(slot, slot, hc_send.at[c, d], hc_recv.at[c, d], plane(d)).wait_recv()
-
-            @pl.when(jnp.logical_not(is_far(head * share + sl)))
-            def _():
+        @pl.when(is_far(head * share + sl))
+        def _():
+            for c in range(2):
+                for k in range(inner - 1):
+                    slot = result.at[sl, block(k), :, columns(c)]
+                    remote(slot, slot, hc_send.at[c, k], hc_recv.at[c, k], plane(1)).wait_recv()
+
+        @pl.when(jnp.logical_not(is_far(head * share + sl)))
+        def _():
+            for d in range(1, inner):
                 slot = result.at[sl, from_mate(d)]
                 remote(slot, slot, c_send.at[sl, d], c_recv.at[sl, d], plane(d)).wait_recv()
 
@@ -931,14 +979,17 @@
         for copy in kv_copies(d):
             copy.wait_send()
         q_copy(d).wait_send()
-        for sl in range(share):
-            @pl.when(is_far(head * share + sl))
-            def _():
-                for c in range(2):
-                    c_copy(sl, d, c).wait_send()
-
-            @pl.when(jnp.logical_not(is_far(head * share + sl)))
-            def _():
+
+    for sl in range(share):
+        @pl.when(is_far(head * share + sl))
+        def _():
+            for c in range(2):
+                for k in range(inner - 1):
+                    far_copy(head * share + sl, c, k).wait_send()
+
+        @pl.when(jnp.logical_not(is_far(head * share + sl)))
+        def _():
+            for d in range(1, inner):
                 c_copy(sl, d).wait_send()
 
     for qb in range(inner):
@@ -950,7 +1001,8 @@
         @pl.when((s // share != head) & is_far(s))
         def _():
             for c in range(2):
-                p_copy(s, c).wait_send()
+                for k in range(inner):
+                    far_give(s, c, k).wait_send()
 
         @pl.when((s // share != head) & jnp.logical_not(is_far(s)))
         def _():
@@ -1020,17 +1072,19 @@
     scratch += [dma((inner, inner))] * 2 + [dma((outer,)), dma((heads, share))] + [dma((share, inner))] * 2 + [dma((4,))]
     shape = (inner, outer, heads, group, back, span, last)
     vmem = pl.BlockSpec(memory_space=pltpu.VMEM)
-    run, last_in, last_spec = kernel, starts, vmem
+    run, last_in, last_spec, first_spec = kernel, starts, vmem, vmem
     if inner == 4 and outer == 4 and back == 3:
         run, last_in, last_spec = square_kernel, doc_lengths, pl.BlockSpec(memory_space=pltpu.SMEM)
-        scratch = [pltpu.VMEM((inner, 1, tok), jnp.int32)] + scratch[:15]
+        ins = [pltpu.VMEM(a.shape, bf16) for a in (queries, keys, values, out_weight)]
+        scratch = ins + [pltpu.VMEM((inner, 1, tok), jnp.int32)] + scratch[:15]
         scratch += [dma((inner,))] * 6 + [dma((back + 1,))] * 4 + [dma((outer, 2))] * 4
         scratch += [dma((inner, 2))] * 4 + [dma((outer,)), dma((heads, share))] + [dma((share, inner))] * 2
-        scratch += [dma((2,))] * 2 + [dma((2, inner))] * 2 + [dma((4,))]
+        scratch += [dma((2, inner))] * 4 + [dma((4,)), dma((4,))]
+        first_spec = pl.BlockSpec(memory_space=pl.ANY)
     return pl.pallas_call(
         functools.partial(run, shape),
-        out_shape=jax.ShapeDtypeStruct((tok, share * inner * wide), bf16),
-        in_specs=[vmem] * 4 + [last_spec],
+        out_shape=pltpu.VMEM((tok, share * inner * wide), bf16),
+        in_specs=[first_spec] * 4 + [last_spec],
         out_specs=vmem,
         scratch_shapes=scratch,
         compiler_params=pltpu.CompilerParams(

time: 109 us -> 105 us (0.963)
  Pallas kernels: 106 us -> 104 us
  local copies, waits for them, and re-layouts: 2.3 us -> 0.97 us
    pallas_call x1, Pallas kernels: 106 us -> 104 us  [body(): pl.pallas_call(functools.partial(run, shape), out_shape=pltpu.VMEM((tok,...]
    unnamed x1, local copies, waits for them, and re-layouts: 2.3 us -> 0.97 us
where the time goes in v3:
time: 105 us
  Pallas kernels  104 us (99%)
    pallas_call x1, Pallas kernels, body(): pl.pallas_call(functools.partial(run, shape), out_shape=pltpu.VMEM((tok,...  104 us

profile of v3, /device:TPU:24, one launch (start us, length us, event | category | flops | bytes accessed | tf_op | source)
XLA Modules:
  0.0 105.2 jit_solution(3472439741621991475)
XLA Ops:
  0.0 104.2 %shard_map.55 = bf16[256,2048]{1,0:T(8,128)(2,1)S(1)} custom-call(bf16[256,16,128]{2,1,0:T(8,128)(2,1)} %q_hbm.1, bf16[256,4,128]{2,1,0:T(4,128)(2,1)} %k_hbm.1, bf16[256,4,128]{2,1,0:T(4,128)(2,1)} %v_hbm.1, bf16[2048,256]{1,0:T(8,128)(2,1)} %w_hbm.1, s32[16]{0:T(128)} %doc_ref.1), custom_call_target="tpu_custom_call" | custom-call | tf_op jit(solution)/shard_map/pallas_call | solution.py:1084
  104.2 1.0 copy.7

commit v4 on v3

--- a/solution.py
+++ b/solution.py
@@ -485,7 +485,7 @@
     q_hbm, k_hbm, v_hbm, w_hbm, doc_ref, out_ref,
     q_in, k_in, v_in, w_ref, lo_ref,
     q_ref, k_ref, v_ref,
-    q_all, k_all, v_all, w_all, a_all, acc, row_max, row_total, partial, peer, summed, result,
+    q_all, k_all, v_all, w_all, a_all, acc, row_max, row_total, partial, peer, summed, result, ahead,
     q_send, q_recv, k_send, k_recv, v_send, v_recv, kz_send, kz_recv, vz_send, vz_recv,
     up_send, up_recv, down_send, down_recv, a_send, a_recv, g_send, g_recv, p_send, p_recv, c_send, c_recv,
     hp_send, hp_recv, hc_send, hc_recv, in_sem, local_sem,
@@ -554,6 +554,30 @@
     def slot_down(t, c):
         return w_all.at[jnp.minimum(o + t, outer - 1), :, pl.ds(c * half, half)]
 
+    rows_half = w_ref.shape[0] // 2
+
+    def tops(slot, t, r, send, recv, to):
+        there = slot(t - 1, 1).at[pl.ds(r * rows_half, rows_half)]
+        k = t * (1 - r)
+        return remote(there, there, send.at[k, 1], recv.at[k, 1], to)
+
+    def last_up(r):
+        return tops(slot_up, outer - 1, r, up_send, up_recv, above)
+
+    def last_down(r):
+        return tops(slot_down, outer - 1, r, down_send, down_recv, below)
+
+    def got_last(r):
+        k = (outer - 1) * (1 - r)
+        for gone, slot, send, recv, by in (
+            (o >= outer - 1, slot_up, up_send, up_recv, below),
+            (o + outer - 1 < outer, slot_down, down_send, down_recv, above),
+        ):
+            @pl.when(gone)
+            def _():
+                here = slot(outer - 1, 1).at[pl.ds(r * rows_half, rows_half)]
+                remote(here, here, send.at[k, 1], recv.at[k, 1], by).wait_recv()
+
     def up_copy(t, c):
         src = w_ref.at[:, pl.ds(c * half, half)] if t == 1 else slot_up(t - 1, c)
         return remote(src, slot_up(t - 1, c), up_send.at[t, c], up_recv.at[t, c], above)
@@ -575,12 +599,20 @@
     def go_up(t, c):
         @pl.when(has_above & (o >= t - 1))
         def _():
-            up_copy(t, c).start()
+            if t == outer - 1 and c == 1:
+                for r in range(2):
+                    last_up(r).start()
+            else:
+                up_copy(t, c).start()
 
     def go_down(t, c):
         @pl.when(has_below & (o + t - 1 < outer))
         def _():
-            down_copy(t, c).start()
+            if t == outer - 1 and c == 1:
+                for r in range(2):
+                    last_down(r).start()
+            else:
+                down_copy(t, c).start()
 
     def pass_up(t, c):
         got_up(t, c)
@@ -806,13 +838,17 @@
         pass_rows(qb)
     pass_up(2, 1)
 
-    def multiply(qb, s, cols=slice(None)):
-        value = jnp.dot(a_all[qb, 0], w_all[s, 0:part_rows, cols], preferred_element_type=jnp.float32)
-        for j in range(1, inner):
-            value += jnp.dot(
+    def product(qb, s, cols, begin, end):
+        value = None
+        for j in range(begin, end):
+            term = jnp.dot(
                 a_all[qb, j], w_all[s, j * part_rows : (j + 1) * part_rows, cols], preferred_element_type=jnp.float32
             )
-        partial[s, qb, :, cols] = value.astype(jnp.bfloat16)
+            value = term if value is None else value + term
+        return value
+
+    def multiply(qb, s, cols=slice(None)):
+        partial[s, qb, :, cols] = product(qb, s, cols, 0, inner).astype(jnp.bfloat16)
 
     def columns(c):
         return pl.ds(0, 2 * half) if c is None else pl.ds(c * half, half)
@@ -930,14 +966,31 @@
     lax.fori_loop(0, near_count, final_block, 0)
     near(near_count - 1, absorb)
     for c in range(2):
-        got_down(outer - 1, c)
-        got_up(outer - 1, c)
+        if c == 0:
+            got_down(outer - 1, c)
+            got_up(outer - 1, c)
+        else:
+            got_last(0)
+
+            def begin(s):
+                def rows(k, carry):
+                    ahead[k] = product(block(k), s, columns(1), 0, inner // 2)
+                    return carry
+
+                lax.fori_loop(0, inner, rows, 0)
+
+            near(outer - 1, begin)
+            got_last(1)
 
         def far(s):
             def rows(k, carry):
                 @pl.when(k < inner)
                 def _():
-                    multiply(block(k), s, columns(c))
+                    if c == 0:
+                        multiply(block(k), s, columns(c))
+                    else:
+                        value = ahead[k] + product(block(k), s, columns(c), inner // 2, inner)
+                        partial[s, block(k), :, columns(c)] = value.astype(jnp.bfloat16)
 
                 @pl.when((k < inner) & (s // share != head))
                 def _():
@@ -1022,11 +1075,19 @@
         for c in range(2):
             @pl.when(has_above & (o >= t - 1))
             def _():
-                up_copy(t, c).wait_send()
+                if t == outer - 1 and c == 1:
+                    for r in range(2):
+                        last_up(r).wait_send()
+                else:
+                    up_copy(t, c).wait_send()
 
             @pl.when(has_below & (o + t - 1 < outer))
             def _():
-                down_copy(t, c).wait_send()
+                if t == outer - 1 and c == 1:
+                    for r in range(2):
+                        last_down(r).wait_send()
+                else:
+                    down_copy(t, c).wait_send()
 
 
 def body(queries, keys, values, out_weight, doc_lengths):
@@ -1077,6 +1138,7 @@
         run, last_in, last_spec = square_kernel, doc_lengths, pl.BlockSpec(memory_space=pltpu.SMEM)
         ins = [pltpu.VMEM(a.shape, bf16) for a in (queries, keys, values, out_weight)]
         scratch = ins + [pltpu.VMEM((inner, 1, tok), jnp.int32)] + scratch[:15]
+        scratch += [pltpu.VMEM((inner, tok, wide // 2), f32)]
         scratch += [dma((inner,))] * 6 + [dma((back + 1,))] * 4 + [dma((outer, 2))] * 4
         scratch += [dma((inner, 2))] * 4 + [dma((outer,)), dma((heads, share))] + [dma((share, inner))] * 2
         scratch += [dma((2, inner))] * 4 + [dma((4,)), dma((4,))]

time: 105 us -> 105 us (level)
  no operation moved by 1% of the time
where the time goes in v4:
time: 105 us
  Pallas kernels  104 us (99%)
    pallas_call x1, Pallas kernels, body(): pl.pallas_call(functools.partial(run, shape), out_shape=pltpu.VMEM((tok,...  104 us

profile of v4, /device:TPU:24, one launch (start us, length us, event | category | flops | bytes accessed | tf_op | source)
XLA Modules:
  0.0 104.7 jit_solution(5550963123306211410)
XLA Ops:
  0.0 103.7 %shard_map.55 = bf16[256,2048]{1,0:T(8,128)(2,1)S(1)} custom-call(bf16[256,16,128]{2,1,0:T(8,128)(2,1)} %q_hbm.1, bf16[256,4,128]{2,1,0:T(4,128)(2,1)} %k_hbm.1, bf16[256,4,128]{2,1,0:T(4,128)(2,1)} %v_hbm.1, bf16[2048,256]{1,0:T(8,128)(2,1)} %w_hbm.1, s32[16]{0:T(128)} %doc_ref.1), custom_call_target="tpu_custom_call" | custom-call | tf_op jit(solution)/shard_map/pallas_call | solution.py:1146
  103.7 1.0 copy.7
